TPU v7x, 128 devices: a whole 4x4x4 slice. The times are simulated.
128 devices in a mesh: zg: 2 (over x_lo), xy: 64 (over x_hi, y, z, core).
Axes of the slice: x: 4 (x_hi: 2, x_lo: 2; x = x_hi * 2 + x_lo), y: 4, z: 4, core: 2. Of those that a mesh axis runs over, the one named last changes fastest.
Arguments:
- charges: float32 [262144], P(('zg', 'xy')), may hold values from -12 to 12
- cells: int32 [8, 262144], P(None, ('zg', 'xy')), may hold values from 0 to 786431
- splines: float32 [8, 262144], P(None, ('zg', 'xy')), may hold values from 0.05 to 1
- counts: int32 [128], P(('zg', 'xy')), may hold values from 1024 to 2048, as said below
- green: bfloat16 [512, 4, 384, 384], P(('zg', 'xy')), may hold values from -0.3125 to 0.3125
Outputs:
- potential: float32 [384, 512, 512], P(('zg', 'xy'))
Inputs may be any that keep to these rules, and one draw needn't show every extreme that they name: `counts`: some device has all 2048 slots live in every draw.
All inputs are finite; a program needn't handle non-finite values.
Results may differ from a plain program's by a relative error of at most 0.0041.
Values may be sent and summed in bfloat16 or wider, within the bound.
No kernel may reach another device: no remote copies, remote signals or barrier semaphores. Data moves between devices by JAX's collectives and lax.ppermute only.
A program may use at most 64 MiB of HBM per device.

v0:
```python
import math
import jax
import jax.numpy as jnp
from jax import lax
from jax.sharding import PartitionSpec as P

NX = 512
NY = 512
NZ = 384
KYB = 4


def tables(length):
    index = jnp.arange(length, dtype=jnp.int32)
    product = index[:, None] * index[None, :] % length
    angle = product.astype(jnp.float32) * (2.0 * math.pi / length)
    return (jnp.cos(angle), jnp.sin(angle))


def shards(charges, cells, splines, counts, green):
    groups = lax.axis_size("zg")
    rows = lax.axis_size("xy")
    slab = NZ // (groups * rows)
    slots = charges.shape[0]
    live = (jnp.arange(slots, dtype=jnp.int32) < counts[0]).astype(jnp.float32)
    values = splines * (charges * live)[None, :]
    density = (
        jnp.zeros((slab * NX * NY,), jnp.float32).at[cells.reshape(-1)].add(values.reshape(-1))
    )
    density = density.reshape(slab, NX, NY)
    cos_y, sin_y = tables(NY)
    cos_x, sin_x = tables(NX)
    scale = 1.0 / math.sqrt(NX * NY)
    forward_y = jnp.stack([cos_y, -sin_y], axis=1)
    along = jnp.einsum("zxy,yev->zxev", density, forward_y, precision=lax.Precision.HIGHEST)
    forward_x = jnp.stack(
        [jnp.stack([cos_x, sin_x], axis=1), jnp.stack([-sin_x, cos_x], axis=1)], axis=0
    )
    spectrum = (
        jnp.einsum("cuex,zxev->zcuv", forward_x, along, precision=lax.Precision.HIGHEST) * scale
    ).astype(jnp.bfloat16)
    pencil = lax.all_to_all(spectrum, ("zg", "xy"), split_axis=2, concat_axis=0, tiled=True)
    depth, parts, waves, width = pencil.shape
    blocks = pencil.reshape(depth, parts, waves, KYB, width // KYB)
    mixed = jnp.einsum("abzw,wcabj->zcabj", green, blocks, preferred_element_type=jnp.float32)
    returned = lax.all_to_all(
        mixed.reshape(depth, parts, waves, width).astype(jnp.bfloat16),
        ("zg", "xy"),
        split_axis=0,
        concat_axis=2,
        tiled=True,
    )
    inverse_x = jnp.stack(
        [jnp.stack([cos_x, -sin_x], axis=1), jnp.stack([sin_x, cos_x], axis=1)], axis=1
    )
    upper_x = inverse_x.astype(jnp.bfloat16)
    lower_x = (inverse_x - upper_x.astype(jnp.float32)).astype(jnp.bfloat16)
    middle = jnp.einsum("xceu,zeuv->zxcv", upper_x, returned, preferred_element_type=jnp.float32)
    middle = middle + jnp.einsum(
        "xceu,zeuv->zxcv", lower_x, returned, preferred_element_type=jnp.float32
    )
    inverse_y = jnp.stack([cos_y, -sin_y], axis=0)
    potential = (
        jnp.einsum("zxcv,cvy->zxy", middle, inverse_y, precision=lax.Precision.HIGHEST) * scale
    )
    return potential


def solution(mesh):
    in_specs = (
        P(("zg", "xy")),
        P(None, ("zg", "xy")),
        P(None, ("zg", "xy")),
        P(("zg", "xy")),
        P(("zg", "xy"), None, None, None),
    )
    out_specs = P(("zg", "xy"), None, None)
    return jax.shard_map(shards, mesh=mesh, in_specs=in_specs, out_specs=out_specs, check_vma=False)
```

profile of v0, /device:TPU:1, one launch (start us, length us, event | category | flops | bytes accessed | tf_op | source)
XLA Modules:
  0.0 296.6 jit_solution(15891612420639336365)
XLA Ops:
  0.0 0.0 copy-start.9
  0.0 0.0 copy-start.7
  0.0 0.0 copy-start.8
  0.0 5.0 %fusion.51 = (f32[512,1,512]{2,0,1:T(8,128)}, f32[512,1,512]{2,0,1:T(8,128)}) fusion(), kind=kLoop, calls=%fused_computation.61 | loop fusion | flops 3670016 | bytes 2097152 | tf_op jit(solution)/shard_map/sin | solution.py:17
  5.0 4.6 %fusion.53 = f32[512,1,512]{2,0,1:T(8,128)} fusion(), kind=kLoop, calls=%fused_computation.63 | loop fusion | flops 3932160 | bytes 1048576 | tf_op jit(solution)/shard_map/neg | solution.py:34
  10.2 0.0 copy-done.9
  10.3 0.0 copy-done.7
  10.3 0.0 copy-done.8
  10.3 0.1 copy.48
  10.4 0.1 compare_select_fusion
  10.5 86.7 %scatter_custom_fusion = f32[786432]{0:T(1024)S(1)} fusion(s32[16384]{0:T(1024)S(1)} %bitcast.109, f32[16384]{0:T(1024)S(1)} %bitcast.108, f32[]{:T(128)} %constant.24.clone.1), kind=kCustom, calls=%fused_computation.45 | custom fusion | flops 16384 | bytes 3145732 | tf_op jit(solution)/shard_map/scatter-add | solution.py:28
  97.2 2.3 reshape.202
  99.5 0.0 copy-start
  99.5 0.0 copy-start.1
  99.5 0.0 copy-start.2
  99.5 6.1 %fusion.35 = (f32[512,1,2,512]{3,0,2,1:T(8,128)}, f32[1,512,2,512]{3,1,2,0:T(8,128)S(1)}, f32[1,512,2,512]{3,1,2,0:T(8,128)S(1)}, f32[512,1,2,512]{3,0,2,1:T(8,128)}) fusion(f32[512,1,512]{2,0,1:T(8,128)} %fusion.53, f32[512,1,512]{2,0,1:T(8,128)} %get-tuple-element.12, f32[512,1,512]{2,0,1:T(8,128)} %get-tuple-element.11), kind=kLoop, calls=%fused_computation.38 | loop fusion | flops 2097152 | bytes 11534336 | tf_op jit(solution)/shard_map/stack | solution.py:53
  105.6 0.0 copy-done
  105.6 0.0 copy-done.1
  105.6 0.0 copy-done.2
  105.6 10.1 %fusion.12 = f32[3,512,2,512]{1,3,2,0:T(8,128)S(1)} fusion(f32[3,512,512,1]{2,1,0,3:T(8,128)S(1)} %copy-done, f32[512,1,512]{2,0,1:T(8,128)S(1)} %copy-done.1, f32[512,1,512]{2,0,1:T(8,128)S(1)} %copy-done.2), kind=kOutput, calls=%fused_computation.19 | convolution fusion | flops 9664200704 | bytes 11534336 | tf_op jit(solution)/shard_map/zxy,yev->zxev/dot_general | solution.py:35
  115.8 22.1 %fusion.11 = bf16[3,2,512,512]{2,3,1,0:T(8,128)(2,1)} fusion(f32[1,512,2,512]{3,1,2,0:T(8,128)S(1)} %get-tuple-element.6, f32[1,512,2,512]{3,1,2,0:T(8,128)S(1)} %get-tuple-element.9, f32[3,512,2,512]{1,3,2,0:T(8,128)S(1)} %fusion.12), kind=kOutput, calls=%fused_computation.17 | convolution fusion | flops 19331547136 | bytes 13631488 | tf_op jit(solution)/shard_map/cuex,zxev->zcuv/dot_general | solution.py:40
  137.8 7.3 %copy.22 = bf16[3,2,512,512]{3,1,0,2:T(2,128)(2,1)S(1)} copy(bf16[3,2,512,512]{2,3,1,0:T(8,128)(2,1)} %fusion.11) | data formatting | bytes 6291456 | tf_op jit(solution)/shard_map/convert_element_type | solution.py:41
  145.2 53.2 %all_to_all.33 = bf16[3,2,512,512]{3,1,0,2:T(2,128)(2,1)S(1)} all-to-all(bf16[3,2,512,512]{3,1,0,2:T(2,128)(2,1)S(1)} %copy.22), channel_id=1, replica_groups=mesh['zg'=2,'xy'=64] {'zg','xy'}, dimensions={2} | all-to-all | bytes 6291456 | tf_op jit(solution)/shard_map/all_to_all | solution.py:42
  198.4 3.3 %copy.24 = bf16[128,3,2,4,512]{4,3,2,1,0:T(4,128)(2,1)} copy(bf16[128,3,2,4,512]{4,2,1,3,0:T(2,128)(2,1)S(1)} %bitcast.103) | data formatting | bytes 6291456 | tf_op jit(solution)/shard_map/all_to_all | solution.py:42
  201.6 4.0 %reshape.193 = bf16[384,2,4,4,128]{4,3,2,1,0:T(4,128)(2,1)S(1)} reshape(bf16[128,3,2,4,512]{4,3,2,1,0:T(4,128)(2,1)} %copy.24) | data formatting | bytes 6291456 | tf_op jit(solution)/shard_map/reshape | solution.py:44
  205.7 5.4 %convert_bitcast_fusion = bf16[384,2,4,4,128]{0,4,1,3,2:T(8,128)(2,1)S(1)} fusion(bf16[4,4,384,384]{3,2,1,0:T(8,128)(2,1)} %param.9, bf16[384,2,4,4,128]{4,3,2,1,0:T(4,128)(2,1)S(1)} %reshape.193), kind=kOutput, calls=%fused_computation.22 | convolution fusion | flops 1209532416 | bytes 11010048 | tf_op jit(solution)/shard_map/abzw,wcabj->zcabj/dot_general | solution.py:45
  211.1 0.4 copy.26
  211.5 4.4 %copy.27 = bf16[384,2,4,512]{3,2,1,0:T(4,128)(2,1)} copy(bf16[384,2,4,512]{0,3,2,1:T(8,128)(2,1)S(1)} %bitcast.104) | data formatting | bytes 6291456 | tf_op jit(solution)/shard_map/convert_element_type | solution.py:47
  215.8 4.8 %all-to-all-start.1 = ((bf16[384,2,4,512]{3,2,1,0:T(4,128)(2,1)}), bf16[384,2,4,512]{3,2,1,0:T(4,128)(2,1)S(1)}, u32[]{:S(2)}, u32[]{:S(2)}) async-start(bf16[384,2,4,512]{3,2,1,0:T(4,128)(2,1)} %copy.27), calls=%async_computation.1 | async-start | bytes 6291456 | tf_op jit(solution)/shard_map/all_to_all | solution.py:46
  220.6 5.0 %sine_negate_fusion = (f32[1,512,512]{2,1,0:T(8,128)}, f32[1,512,512]{2,1,0:T(8,128)}) fusion(), kind=kLoop, calls=%fused_computation.53 | loop fusion | flops 3932160 | bytes 2097152 | tf_op jit(solution)/shard_map/neg | solution.py:34
  225.6 36.8 %all-to-all-done.1 = bf16[384,2,4,512]{3,2,1,0:T(4,128)(2,1)S(1)} async-done(((bf16[384,2,4,512]{3,2,1,0:T(4,128)(2,1)}), bf16[384,2,4,512]{3,2,1,0:T(4,128)(2,1)S(1)}, u32[]{:S(2)}, u32[]{:S(2)}) %all-to-all-start.1) | async-done | bytes 3145760 | tf_op jit(solution)/shard_map/all_to_all | solution.py:46
  262.4 4.9 %copy.28 = bf16[3,2,128,4,512]{4,1,3,2,0:T(2,128)(2,1)} copy(bf16[3,2,128,4,512]{4,3,1,0,2:T(4,128)(2,1)S(1)} %bitcast.102) | data formatting | bytes 6291456 | tf_op jit(solution)/shard_map/all_to_all | solution.py:46
  267.3 7.0 %copy.37 = bf16[3,2,512,512,1]{2,3,1,4,0:T(8,128)(2,1)S(1)} copy(bf16[3,2,512,512,1]{3,1,2,0,4:T(2,128)(2,1)} %bitcast.105) | data formatting | bytes 6291456 | tf_op jit(solution)/shard_map/all_to_all | solution.py:46
  274.3 0.0 copy-start.5
  274.3 0.0 copy-start.6
  274.3 6.5 %fusion.22 = f32[3,512,512,2,1]{2,1,4,3,0:T(8,128)S(1)} fusion(bf16[3,2,512,512,1]{2,3,1,4,0:T(8,128)(2,1)S(1)} %copy.37, f32[512,1,2,512]{3,0,2,1:T(8,128)} %get-tuple-element.10, f32[512,1,2,512]{3,0,2,1:T(8,128)} %get-tuple-element.5), kind=kOutput, calls=%fused_computation.28 | convolution fusion | flops 3225419776 | bytes 13631488 | tf_op jit(solution)/shard_map/xceu,zeuv->zxcv/dot_general | solution.py:58
  280.8 0.0 copy-done.5
  280.8 0.0 copy-done.6
  280.8 0.0 copy-start.3
  280.9 0.0 copy-start.4
  280.9 3.5 %fusion.28 = f32[3,512,512,2,1]{2,1,4,3,0:T(8,128)S(1)} fusion(bf16[3,2,512,512,1]{2,3,1,4,0:T(8,128)(2,1)S(1)} %copy.37, f32[512,1,2,512]{3,0,2,1:T(8,128)S(1)} %copy-done.6, f32[512,1,2,512]{3,0,2,1:T(8,128)S(1)} %copy-done.5), kind=kOutput, calls=%fused_computation.33 | convolution fusion | flops 3226468352 | bytes 13631488 | tf_op jit(solution)/shard_map/xceu,zeuv->zxcv/dot_general | solution.py:59
  284.3 0.0 copy-done.3
  284.4 0.0 copy-done.4
  284.4 12.0 %bitcast_multiply_fusion.1 = f32[3,512,512]{2,1,0:T(8,128)} fusion(f32[1,512,512]{2,1,0:T(8,128)S(1)} %copy-done.3, f32[1,512,512]{2,1,0:T(8,128)S(1)} %copy-done.4, f32[3,512,512,2,1]{2,1,4,3,0:T(8,128)S(1)} %fusion.28, f32[3,512,512,2,1]{2,1,4,3,0:T(8,128)S(1)} %fusion.22), kind=kOutput, calls=%fused_computation.18 | convolution fusion | flops 9666560000 | bytes 17825792 | tf_op jit(solution)/shard_map/zxcv,cvy->zxy/dot_general | solution.py:64
  (3 shorter events, 0.0 us)
Async XLA Ops:
  0.0 10.2 %copy-start.9 = (f32[2048]{0:T(1024)S(1)}, f32[2048]{0:T(1024)}, u32[]{:S(2)}) copy-start(f32[2048]{0:T(1024)} %param.5) | copy-start | bytes 24580
  0.0 10.3 %copy-start.7 = (f32[8,2048]{1,0:T(8,128)S(1)}, f32[8,2048]{1,0:T(8,128)}, u32[]{:S(2)}) copy-start(f32[8,2048]{1,0:T(8,128)} %param.7) | copy-start | bytes 196612
  0.0 10.3 %copy-start.8 = (s32[8,2048]{1,0:T(8,128)S(1)}, s32[8,2048]{1,0:T(8,128)}, u32[]{:S(2)}) copy-start(s32[8,2048]{1,0:T(8,128)} %param.6) | copy-start | bytes 196612
  99.5 6.1 %copy-start = (f32[3,512,512,1]{2,1,0,3:T(8,128)S(1)}, f32[3,512,512,1]{2,1,0,3:T(8,128)}, u32[]{:S(2)}) copy-start(f32[3,512,512,1]{2,1,0,3:T(8,128)} %reshape.202) | copy-start | bytes 9437188
  99.5 6.1 %copy-start.1 = (f32[512,1,512]{2,0,1:T(8,128)S(1)}, f32[512,1,512]{2,0,1:T(8,128)}, u32[]{:S(2)}) copy-start(f32[512,1,512]{2,0,1:T(8,128)} %get-tuple-element.12) | copy-start | bytes 3145732
  99.5 6.1 %copy-start.2 = (f32[512,1,512]{2,0,1:T(8,128)S(1)}, f32[512,1,512]{2,0,1:T(8,128)}, u32[]{:S(2)}) copy-start(f32[512,1,512]{2,0,1:T(8,128)} %fusion.53) | copy-start | bytes 3145732
  215.8 46.5 %all-to-all-start.1 = ((bf16[384,2,4,512]{3,2,1,0:T(4,128)(2,1)}), bf16[384,2,4,512]{3,2,1,0:T(4,128)(2,1)S(1)}, u32[]{:S(2)}, u32[]{:S(2)}) async-start(bf16[384,2,4,512]{3,2,1,0:T(4,128)(2,1)} %copy.27), calls=%async_computation.1 | async-start | bytes 6291456 | tf_op jit(solution)/shard_map/all_to_all | solution.py:46
  274.3 6.5 %copy-start.5 = (f32[512,1,2,512]{3,0,2,1:T(8,128)S(1)}, f32[512,1,2,512]{3,0,2,1:T(8,128)}, u32[]{:S(2)}) copy-start(f32[512,1,2,512]{3,0,2,1:T(8,128)} %get-tuple-element.5) | copy-start | bytes 6291460
  274.3 6.5 %copy-start.6 = (f32[512,1,2,512]{3,0,2,1:T(8,128)S(1)}, f32[512,1,2,512]{3,0,2,1:T(8,128)}, u32[]{:S(2)}) copy-start(f32[512,1,2,512]{3,0,2,1:T(8,128)} %get-tuple-element.10) | copy-start | bytes 6291460
  280.8 3.5 %copy-start.3 = (f32[1,512,512]{2,1,0:T(8,128)S(1)}, f32[1,512,512]{2,1,0:T(8,128)}, u32[]{:S(2)}) copy-start(f32[1,512,512]{2,1,0:T(8,128)} %get-tuple-element.13) | copy-start | bytes 3145732
  280.9 3.5 %copy-start.4 = (f32[1,512,512]{2,1,0:T(8,128)S(1)}, f32[1,512,512]{2,1,0:T(8,128)}, u32[]{:S(2)}) copy-start(f32[1,512,512]{2,1,0:T(8,128)} %get-tuple-element.14) | copy-start | bytes 3145732
where the time goes:
time: 301 us; the launch traced here: 297 us
  other arithmetic  108 us (36%)
  matrix products  59.6 us (20%)
  blocking collectives  53.2 us (18%)
  waiting for transfers between devices  36.8 us (12%)
  local copies, waits for them, and re-layouts  33.7 us (11%)
  starting transfers between devices  4.78 us (2%)
    scatter-add x1, other arithmetic, shards(): jnp.zeros((slab * NX * NY,), jnp.float32).at[cells.reshape(-1)]  86.7 us
    all_to_all x1, blocking collectives, shards(): lax.all_to_all(spectrum, ('zg', 'xy'), split_axis=2, concat_axis=0, tiled...  53.2 us
    all_to_all x1, waiting for transfers between devices, shards(): lax.all_to_all(mixed.reshape(depth, parts, waves, width).astype(jnp.bfloa...  36.8 us
    dot_general x1, matrix products, shards(): jnp.einsum('cuex,zxev->zcuv', forward_x, along, precision=lax.Precision.H...  22.1 us
    dot_general x1, matrix products, shards(): jnp.einsum('zxcv,cvy->zxy', middle, inverse_y, precision=lax.Precision.HI...  12 us
    all_to_all x2, local copies, waits for them, and re-layouts, shards(): lax.all_to_all(mixed.reshape(depth, parts, waves, width).astype(jnp.bfloa...  11.9 us
    dot_general x1, matrix products, shards(): jnp.einsum('zxy,yev->zxev', density, forward_y, precision=lax.Precision.H...  10.1 us
    neg x2, other arithmetic, shards(): forward_y = jnp.stack([cos_y, -sin_y], axis=1)  9.62 us
  transfers between devices with their start and end apart: 1, of which 1 were waited for; matrix products, arithmetic and copies ran while one was open for 2% of the time, Pallas kernels for 0%

commit v1 on v0

--- a/solution.py
+++ b/solution.py
@@ -39,7 +39,12 @@
     spectrum = (
         jnp.einsum("cuex,zxev->zcuv", forward_x, along, precision=lax.Precision.HIGHEST) * scale
     ).astype(jnp.bfloat16)
-    pencil = lax.all_to_all(spectrum, ("zg", "xy"), split_axis=2, concat_axis=0, tiled=True)
+    pencil = jnp.concatenate(
+        lax.all_to_all(
+            jnp.stack(jnp.split(spectrum, lax.axis_size(("zg", "xy")), axis=2)), ("zg", "xy"), 0, 0
+        ),
+        axis=0,
+    )
     depth, parts, waves, width = pencil.shape
     blocks = pencil.reshape(depth, parts, waves, KYB, width // KYB)
     mixed = jnp.einsum("abzw,wcabj->zcabj", green, blocks, preferred_element_type=jnp.float32)

time: 301 us -> 293 us (0.973)
  local copies, waits for them, and re-layouts: 33.7 us -> 25.7 us
    convert_element_type x1 -> x0, local copies, waits for them, and re-layouts: 7.3 us -> none  [shards(): spectrum = (jnp.einsum('cuex,zxev->zcuv', forward_x, along, precision=lax...]
    another operation x0 -> x2, local copies, waits for them, and re-layouts: none -> 4.05 us  [the longest x1 4.03 us: shards(): blocks = pencil.reshape(depth, parts, waves, KYB, width // KYB)]
    reshape x1 -> x0, local copies, waits for them, and re-layouts: 4.03 us -> none  [shards(): blocks = pencil.reshape(depth, parts, waves, KYB, width // KYB)]
    all_to_all x1 -> x0, local copies, waits for them, and re-layouts: 3.28 us -> none  [shards(): lax.all_to_all(spectrum, ('zg', 'xy'), split_axis=2, concat_axis=0, tiled...]
where the time goes in v1:
time: 293 us; the launch traced here: 289 us
  other arithmetic  108 us (37%)
  matrix products  59.2 us (20%)
  blocking collectives  53.2 us (18%)
  waiting for transfers between devices  36.7 us (13%)
  local copies, waits for them, and re-layouts  25.7 us (9%)
  starting transfers between devices  4.88 us (2%)
    scatter-add x1, other arithmetic, shards(): jnp.zeros((slab * NX * NY,), jnp.float32).at[cells.reshape(-1)]  86.7 us
    all_to_all x1, blocking collectives, shards(): lax.all_to_all(jnp.stack(jnp.split(spectrum, lax.axis_size(('zg', 'xy')),...  53.2 us
    all_to_all x1, waiting for transfers between devices, shards(): lax.all_to_all(mixed.reshape(depth, parts, waves, width).astype(jnp.bfloa...  36.7 us
    dot_general x1, matrix products, shards(): jnp.einsum('cuex,zxev->zcuv', forward_x, along, precision=lax.Precision.H...  21.6 us
    dot_general x1, matrix products, shards(): jnp.einsum('zxcv,cvy->zxy', middle, inverse_y, precision=lax.Precision.HI...  12 us
    all_to_all x2, local copies, waits for them, and re-layouts, shards(): lax.all_to_all(mixed.reshape(depth, parts, waves, width).astype(jnp.bfloa...  11.9 us
    dot_general x1, matrix products, shards(): jnp.einsum('zxy,yev->zxev', density, forward_y, precision=lax.Precision.H...  10.3 us
    neg x2, other arithmetic, shards(): forward_y = jnp.stack([cos_y, -sin_y], axis=1)  9.67 us
  transfers between devices with their start and end apart: 1, of which 1 were waited for; matrix products, arithmetic and copies ran while one was open for 2% of the time, Pallas kernels for 0%

profile of v1, /device:TPU:1, one launch (start us, length us, event | category | flops | bytes accessed | tf_op | source)
XLA Modules:
  0.0 288.9 jit_solution(14390799122390987239)
XLA Ops:
  0.0 0.0 copy-start.9
  0.0 0.0 copy-start.7
  0.0 0.0 copy-start.8
  0.0 5.0 %fusion.51 = (f32[512,1,512]{2,0,1:T(8,128)}, f32[512,1,512]{2,0,1:T(8,128)}) fusion(), kind=kLoop, calls=%fused_computation.61 | loop fusion | flops 3670016 | bytes 2097152 | tf_op jit(solution)/shard_map/sin | solution.py:17
  5.0 4.6 %fusion.53 = f32[512,1,512]{2,0,1:T(8,128)} fusion(), kind=kLoop, calls=%fused_computation.63 | loop fusion | flops 3932160 | bytes 1048576 | tf_op jit(solution)/shard_map/neg | solution.py:34
  10.3 0.0 copy-done.9
  10.3 0.0 copy-done.7
  10.3 0.0 copy-done.8
  10.4 0.1 copy.38
  10.4 0.1 compare_select_fusion
  10.5 86.7 %scatter_custom_fusion = f32[786432]{0:T(1024)S(1)} fusion(s32[16384]{0:T(1024)S(1)} %bitcast.617, f32[16384]{0:T(1024)S(1)} %bitcast.616, f32[]{:T(128)} %constant.24.clone.1), kind=kCustom, calls=%fused_computation.45 | custom fusion | flops 16384 | bytes 3145732 | tf_op jit(solution)/shard_map/scatter-add | solution.py:28
  97.2 2.3 reshape.197
  99.5 0.0 copy-start
  99.5 0.0 copy-start.1
  99.5 0.0 copy-start.2
  99.5 6.2 %fusion.35 = (f32[512,1,2,512]{3,0,2,1:T(8,128)}, f32[1,512,2,512]{3,1,2,0:T(8,128)S(1)}, f32[1,512,2,512]{3,1,2,0:T(8,128)S(1)}, f32[512,1,2,512]{3,0,2,1:T(8,128)}) fusion(f32[512,1,512]{2,0,1:T(8,128)} %fusion.53, f32[512,1,512]{2,0,1:T(8,128)} %get-tuple-element.12, f32[512,1,512]{2,0,1:T(8,128)} %get-tuple-element.11), kind=kLoop, calls=%fused_computation.38 | loop fusion | flops 2097152 | bytes 11534336 | tf_op jit(solution)/shard_map/stack | solution.py:58
  105.7 0.0 copy-done
  105.7 0.0 copy-done.1
  105.7 0.0 copy-done.2
  105.7 10.3 %fusion.12 = f32[3,512,2,512]{3,1,2,0:T(8,128)S(1)} fusion(f32[3,512,512,1]{2,1,0,3:T(8,128)S(1)} %copy-done, f32[512,1,512]{2,0,1:T(8,128)S(1)} %copy-done.1, f32[512,1,512]{2,0,1:T(8,128)S(1)} %copy-done.2), kind=kOutput, calls=%fused_computation.19 | convolution fusion | flops 9664200704 | bytes 11534336 | tf_op jit(solution)/shard_map/zxy,yev->zxev/dot_general | solution.py:35
  116.0 21.6 %fusion.11 = bf16[3,2,512,512]{3,2,1,0:T(8,128)(2,1)S(1)} fusion(f32[1,512,2,512]{3,1,2,0:T(8,128)S(1)} %get-tuple-element.6, f32[1,512,2,512]{3,1,2,0:T(8,128)S(1)} %get-tuple-element.9, f32[3,512,2,512]{3,1,2,0:T(8,128)S(1)} %fusion.12), kind=kOutput, calls=%fused_computation.17 | convolution fusion | flops 19331547136 | bytes 13631488 | tf_op jit(solution)/shard_map/cuex,zxev->zcuv/dot_general | solution.py:40
  140.7 53.2 %all_to_all.23 = bf16[128,3,2,4,512]{4,3,2,1,0:T(4,128)(2,1)} all-to-all(bf16[128,3,2,4,512]{4,3,2,1,0:T(4,128)(2,1)S(1)} %constant_dynamic-update-slice_fusion), channel_id=1, replica_groups=mesh['zg'=2,'xy'=64] {'zg','xy'}, dimensions={0} | all-to-all | bytes 6291456 | tf_op jit(solution)/shard_map/all_to_all | solution.py:43
  193.9 4.0 %reshape_reshape.3 = bf16[384,2,4,4,128]{4,3,2,1,0:T(4,128)(2,1)S(1)} reshape(bf16[128,3,2,4,512]{4,3,2,1,0:T(4,128)(2,1)} %all_to_all.23) | data formatting | bytes 6291456 | tf_op jit(solution)/shard_map/reshape;reshape | solution.py:49
  197.9 5.4 %convert_bitcast_fusion = bf16[384,2,4,4,128]{0,4,1,3,2:T(8,128)(2,1)S(1)} fusion(bf16[4,4,384,384]{3,2,1,0:T(8,128)(2,1)} %param.9, bf16[384,2,4,4,128]{4,3,2,1,0:T(4,128)(2,1)S(1)} %reshape_reshape.3), kind=kOutput, calls=%fused_computation.22 | convolution fusion | flops 1209532416 | bytes 11010048 | tf_op jit(solution)/shard_map/abzw,wcabj->zcabj/dot_general | solution.py:50
  203.3 0.4 copy.18
  203.7 4.4 %copy.19 = bf16[384,2,4,512]{3,2,1,0:T(4,128)(2,1)} copy(bf16[384,2,4,512]{0,3,2,1:T(8,128)(2,1)S(1)} %bitcast.612) | data formatting | bytes 6291456 | tf_op jit(solution)/shard_map/convert_element_type | solution.py:52
  208.1 4.9 %all-to-all-start.1 = ((bf16[384,2,4,512]{3,2,1,0:T(4,128)(2,1)}), bf16[384,2,4,512]{3,2,1,0:T(4,128)(2,1)S(1)}, u32[]{:S(2)}, u32[]{:S(2)}) async-start(bf16[384,2,4,512]{3,2,1,0:T(4,128)(2,1)} %copy.19), calls=%async_computation.1 | async-start | bytes 6291456 | tf_op jit(solution)/shard_map/all_to_all | solution.py:51
  213.0 5.0 %sine_negate_fusion = (f32[1,512,512]{2,1,0:T(8,128)}, f32[1,512,512]{2,1,0:T(8,128)}) fusion(), kind=kLoop, calls=%fused_computation.53 | loop fusion | flops 3932160 | bytes 2097152 | tf_op jit(solution)/shard_map/neg | solution.py:34
  218.0 36.7 %all-to-all-done.1 = bf16[384,2,4,512]{3,2,1,0:T(4,128)(2,1)S(1)} async-done(((bf16[384,2,4,512]{3,2,1,0:T(4,128)(2,1)}), bf16[384,2,4,512]{3,2,1,0:T(4,128)(2,1)S(1)}, u32[]{:S(2)}, u32[]{:S(2)}) %all-to-all-start.1) | async-done | bytes 3145760 | tf_op jit(solution)/shard_map/all_to_all | solution.py:51
  254.7 4.9 %copy.20 = bf16[3,2,128,4,512]{4,1,3,2,0:T(2,128)(2,1)} copy(bf16[3,2,128,4,512]{4,3,1,0,2:T(4,128)(2,1)S(1)} %bitcast.611) | data formatting | bytes 6291456 | tf_op jit(solution)/shard_map/all_to_all | solution.py:51
  259.6 7.0 %copy.28 = bf16[3,2,512,512,1]{2,3,1,4,0:T(8,128)(2,1)S(1)} copy(bf16[3,2,512,512,1]{3,1,2,0,4:T(2,128)(2,1)} %bitcast.613) | data formatting | bytes 6291456 | tf_op jit(solution)/shard_map/all_to_all | solution.py:51
  266.6 0.0 copy-start.5
  266.7 0.0 copy-start.6
  266.7 6.5 %fusion.22 = f32[3,512,512,2,1]{2,1,4,3,0:T(8,128)S(1)} fusion(bf16[3,2,512,512,1]{2,3,1,4,0:T(8,128)(2,1)S(1)} %copy.28, f32[512,1,2,512]{3,0,2,1:T(8,128)} %get-tuple-element.10, f32[512,1,2,512]{3,0,2,1:T(8,128)} %get-tuple-element.5), kind=kOutput, calls=%fused_computation.28 | convolution fusion | flops 3225419776 | bytes 13631488 | tf_op jit(solution)/shard_map/xceu,zeuv->zxcv/dot_general | solution.py:63
  273.2 0.0 copy-done.5
  273.2 0.0 copy-done.6
  273.2 0.0 copy-start.3
  273.2 0.0 copy-start.4
  273.2 3.5 %fusion.28 = f32[3,512,512,2,1]{2,1,4,3,0:T(8,128)S(1)} fusion(bf16[3,2,512,512,1]{2,3,1,4,0:T(8,128)(2,1)S(1)} %copy.28, f32[512,1,2,512]{3,0,2,1:T(8,128)S(1)} %copy-done.6, f32[512,1,2,512]{3,0,2,1:T(8,128)S(1)} %copy-done.5), kind=kOutput, calls=%fused_computation.33 | convolution fusion | flops 3226468352 | bytes 13631488 | tf_op jit(solution)/shard_map/xceu,zeuv->zxcv/dot_general | solution.py:64
  276.7 0.0 copy-done.3
  276.7 0.0 copy-done.4
  276.7 12.0 %bitcast_multiply_fusion.1 = f32[3,512,512]{2,1,0:T(8,128)} fusion(f32[1,512,512]{2,1,0:T(8,128)S(1)} %copy-done.3, f32[1,512,512]{2,1,0:T(8,128)S(1)} %copy-done.4, f32[3,512,512,2,1]{2,1,4,3,0:T(8,128)S(1)} %fusion.28, f32[3,512,512,2,1]{2,1,4,3,0:T(8,128)S(1)} %fusion.22), kind=kOutput, calls=%fused_computation.18 | convolution fusion | flops 9666560000 | bytes 17825792 | tf_op jit(solution)/shard_map/zxcv,cvy->zxy/dot_general | solution.py:69
  (131 shorter events, 2.7 us)
Async XLA Ops:
  0.0 10.3 %copy-start.9 = (f32[2048]{0:T(1024)S(1)}, f32[2048]{0:T(1024)}, u32[]{:S(2)}) copy-start(f32[2048]{0:T(1024)} %param.5) | copy-start | bytes 24580
  0.0 10.3 %copy-start.7 = (f32[8,2048]{1,0:T(8,128)S(1)}, f32[8,2048]{1,0:T(8,128)}, u32[]{:S(2)}) copy-start(f32[8,2048]{1,0:T(8,128)} %param.7) | copy-start | bytes 196612
  0.0 10.3 %copy-start.8 = (s32[8,2048]{1,0:T(8,128)S(1)}, s32[8,2048]{1,0:T(8,128)}, u32[]{:S(2)}) copy-start(s32[8,2048]{1,0:T(8,128)} %param.6) | copy-start | bytes 196612
  99.5 6.2 %copy-start = (f32[3,512,512,1]{2,1,0,3:T(8,128)S(1)}, f32[3,512,512,1]{2,1,0,3:T(8,128)}, u32[]{:S(2)}) copy-start(f32[3,512,512,1]{2,1,0,3:T(8,128)} %reshape.197) | copy-start | bytes 9437188
  99.5 6.2 %copy-start.1 = (f32[512,1,512]{2,0,1:T(8,128)S(1)}, f32[512,1,512]{2,0,1:T(8,128)}, u32[]{:S(2)}) copy-start(f32[512,1,512]{2,0,1:T(8,128)} %get-tuple-element.12) | copy-start | bytes 3145732
  99.5 6.2 %copy-start.2 = (f32[512,1,512]{2,0,1:T(8,128)S(1)}, f32[512,1,512]{2,0,1:T(8,128)}, u32[]{:S(2)}) copy-start(f32[512,1,512]{2,0,1:T(8,128)} %fusion.53) | copy-start | bytes 3145732
  208.1 46.6 %all-to-all-start.1 = ((bf16[384,2,4,512]{3,2,1,0:T(4,128)(2,1)}), bf16[384,2,4,512]{3,2,1,0:T(4,128)(2,1)S(1)}, u32[]{:S(2)}, u32[]{:S(2)}) async-start(bf16[384,2,4,512]{3,2,1,0:T(4,128)(2,1)} %copy.19), calls=%async_computation.1 | async-start | bytes 6291456 | tf_op jit(solution)/shard_map/all_to_all | solution.py:51
  266.6 6.5 %copy-start.5 = (f32[512,1,2,512]{3,0,2,1:T(8,128)S(1)}, f32[512,1,2,512]{3,0,2,1:T(8,128)}, u32[]{:S(2)}) copy-start(f32[512,1,2,512]{3,0,2,1:T(8,128)} %get-tuple-element.5) | copy-start | bytes 6291460
  266.7 6.5 %copy-start.6 = (f32[512,1,2,512]{3,0,2,1:T(8,128)S(1)}, f32[512,1,2,512]{3,0,2,1:T(8,128)}, u32[]{:S(2)}) copy-start(f32[512,1,2,512]{3,0,2,1:T(8,128)} %get-tuple-element.10) | copy-start | bytes 6291460
  273.2 3.5 %copy-start.3 = (f32[1,512,512]{2,1,0:T(8,128)S(1)}, f32[1,512,512]{2,1,0:T(8,128)}, u32[]{:S(2)}) copy-start(f32[1,512,512]{2,1,0:T(8,128)} %get-tuple-element.13) | copy-start | bytes 3145732
  273.2 3.5 %copy-start.4 = (f32[1,512,512]{2,1,0:T(8,128)S(1)}, f32[1,512,512]{2,1,0:T(8,128)}, u32[]{:S(2)}) copy-start(f32[1,512,512]{2,1,0:T(8,128)} %get-tuple-element.14) | copy-start | bytes 3145732
